TPU v7x, 1024 devices: a whole 4x4x32 slice. The times are simulated.
1024 devices in a mesh: section: 16 (over y, z_hi), ctx: 64 (over z_lo, x, core).
Axes of the slice: x: 4, y: 4, z: 32 (z_hi: 4, z_lo: 8; z = z_hi * 8 + z_lo), core: 2. Of those that a mesh axis runs over, the one named last changes fastest.
Arguments:
- queries: bfloat16 [16, 8, 8192, 512], P('section', None, 'ctx'), may hold values from -5 to 5
- keys: bfloat16 [16, 8, 8192, 128], P('section', None, 'ctx'), may hold values from -5 to 5
- values: bfloat16 [16, 8, 8192, 128], P('section', None, 'ctx'), may hold values from -6 to 6
- out_grad: bfloat16 [16, 8192, 512], P('section', 'ctx'), may hold values from -6 to 6
- stretch_ids: int32 [128], P('ctx'), may hold values from 0 to 127, as said below
- stash_slot: int32 [16], P('section'), may hold values from 0 to 7
Outputs:
- passed_grads: bfloat16 [16, 8192, 768], P('section', 'ctx')
Inputs may be any that keep to these rules, and one draw needn't show every extreme that they name: `stretch_ids`: for each sequence, the entries of its 64 row blocks (two a block, blocks in order) are a permutation of 0 to 127 in which a block's two entries are some c and 127 - c, in either order.
All inputs are finite; a program needn't handle non-finite values.
Results may differ from a plain program's by a relative error of at most 0.035.
Values may be sent and summed in bfloat16 or wider, within the bound.
A program may use at most 64 MiB of HBM per device.

v0:
```python
import math

import jax
import jax.numpy as jnp
from jax import lax
from jax.sharding import Mesh
from jax.sharding import PartitionSpec as P

SEQS = 1
CTX = ("ctx_0", "ctx_1", "ctx_2")


neg_large = -1e30
far_place = 1073741824


def sent_together(arrays, axis, dim, along):
    ends, at = ([], 0)
    for a in arrays[:-1]:
        at += a.shape[along]
        ends.append(at)
    both = jnp.concatenate(arrays, axis=along)
    return tuple(jnp.split(lax.all_gather(both, axis, axis=dim, tiled=True), ends, axis=along))


def split_up(x, dim, peers):
    shape = x.shape
    parts = x.reshape(*shape[:dim], peers, shape[dim] // peers, *shape[dim + 1 :])
    return jnp.moveaxis(parts, dim, 0)


def sum_by_chip(x, chips, core, dim):
    sizes = (lax.axis_size(chips), lax.axis_size(core))
    parts = split_up(x, dim, sizes[0] * sizes[1])
    inside = parts.shape[1:]
    parts = parts.reshape(*sizes, *inside).swapaxes(0, 1).reshape(-1, *inside)
    parts = lax.psum_scatter(parts, core, scatter_dimension=0, tiled=True)
    return lax.psum_scatter(parts, chips, scatter_dimension=0, tiled=True)[0]


def passed_along(value, axis, steps):
    count = lax.axis_size(axis)
    pairs = [(source, (source + steps) % count) for source in range(count)]
    return lax.ppermute(value, axis, pairs)


def token_positions(stretch_numbers, row_count, stretch_size):
    row_ids = jnp.arange(row_count, dtype=jnp.int32)
    matches = (row_ids // stretch_size)[:, None] == jnp.arange(
        stretch_numbers.shape[0], dtype=jnp.int32
    )[None, :]
    stretch_start = jnp.sum(jnp.where(matches, stretch_numbers[None, :], 0), axis=1)
    return stretch_start * stretch_size + row_ids % stretch_size


def block_scores(query_rows, key_block, query_place, key_place, softmax_scale):
    scores = (
        jnp.einsum("thd,cd->thc", query_rows, key_block, preferred_element_type=jnp.float32)
        * softmax_scale
    )
    visible = key_place[None, None, :] <= query_place[:, None, None]
    return (scores, visible)


def forward_block(
    carried, query_rows, key_block, value_block, query_place, key_place, softmax_scale
):
    row_top, row_total, summed = carried
    scores, visible = block_scores(query_rows, key_block, query_place, key_place, softmax_scale)
    new_top = jnp.maximum(row_top, jnp.max(jnp.where(visible, scores, neg_large), axis=2))
    weights = jnp.where(visible, jnp.exp(scores - new_top[:, :, None]), 0.0)
    fading = jnp.exp(row_top - new_top)
    row_total = row_total * fading + jnp.sum(weights, axis=2)
    summed = summed * fading[:, :, None] + jnp.einsum(
        "thc,cd->thd", weights.astype(jnp.bfloat16), value_block, preferred_element_type=jnp.float32
    )
    return (new_top, row_total, summed)


def finish_forward(carried, grad_rows):
    row_top, row_total, summed = carried
    attention = summed / row_total[:, :, None]
    row_delta = jnp.sum(grad_rows.astype(jnp.float32) * attention, axis=2)
    return (row_top + jnp.log(row_total), row_delta)


def backward_block(
    query_rows,
    grad_rows,
    key_block,
    value_block,
    query_place,
    key_place,
    log_total,
    row_delta,
    softmax_scale,
):
    scores, visible = block_scores(query_rows, key_block, query_place, key_place, softmax_scale)
    weights = jnp.where(visible, jnp.exp(scores - log_total[:, :, None]), 0.0)
    probs_half = weights.astype(jnp.bfloat16)
    prob_grad = jnp.einsum(
        "thd,cd->thc", grad_rows, value_block, preferred_element_type=jnp.float32
    )
    score_grad = (softmax_scale * weights * (prob_grad - row_delta[:, :, None])).astype(
        jnp.bfloat16
    )
    query_grad = jnp.einsum(
        "thc,cd->thd", score_grad, key_block, preferred_element_type=jnp.float32
    )
    key_grad = jnp.einsum("thc,thd->cd", score_grad, query_rows, preferred_element_type=jnp.float32)
    value_grad = jnp.einsum(
        "thc,thd->cd", probs_half, grad_rows, preferred_element_type=jnp.float32
    )
    return (query_grad, jnp.concatenate([key_grad, value_grad], axis=1))


def per_device(queries, keys, values, out_grad, stretch_ids, stash_slot):
    stash_index = stash_slot[0]
    query_flat = lax.dynamic_index_in_dim(queries[0], stash_index, 0, keepdims=False)
    key_rows = lax.dynamic_index_in_dim(keys[0], stash_index, 0, keepdims=False)
    value_rows = lax.dynamic_index_in_dim(values[0], stash_index, 0, keepdims=False)
    row_count, head_size = key_rows.shape
    group_size = query_flat.shape[1] // head_size
    stretch_size = row_count // 2
    softmax_scale = 1.0 / math.sqrt(head_size)
    query_rows = query_flat.reshape(row_count, group_size, head_size)
    grad_rows = out_grad[0].reshape(row_count, group_size, head_size)
    query_place = token_positions(stretch_ids, row_count, stretch_size)
    initial = (
        jnp.full((row_count, group_size), neg_large, jnp.float32),
        jnp.zeros((row_count, group_size), jnp.float32),
        jnp.zeros((row_count, group_size, head_size), jnp.float32),
    )
    whole_keys, whole_values, whole_ids = (
        *sent_together((key_rows, value_rows), CTX, 0, 1),
        lax.all_gather(stretch_ids, CTX, axis=0, tiled=True),
    )
    total_rows = whole_keys.shape[0]
    shard_count = total_rows // row_count
    per_step = math.gcd(shard_count, max(1, 512 // row_count))
    step_rows = per_step * row_count
    step_count = shard_count // per_step
    own_seq = lax.axis_index(CTX) % SEQS

    def gathered_block(step_index):
        start = step_index * step_rows
        key_block = lax.dynamic_slice_in_dim(whole_keys, start, step_rows, 0)
        value_block = lax.dynamic_slice_in_dim(whole_values, start, step_rows, 0)
        id_block = lax.dynamic_slice_in_dim(whole_ids, step_index * 2 * per_step, 2 * per_step, 0)
        place = token_positions(id_block, step_rows, stretch_size)
        shard_of_row = (start + jnp.arange(step_rows, dtype=jnp.int32)) // row_count
        place = jnp.where(shard_of_row % SEQS == own_seq, place, far_place)
        return (key_block, value_block, place)

    def forward_step(step_index, carried):
        key_block, value_block, place = gathered_block(step_index)
        return forward_block(
            carried, query_rows, key_block, value_block, query_place, place, softmax_scale
        )

    carried = lax.fori_loop(0, step_count, forward_step, initial)
    log_total, row_delta = finish_forward(carried, grad_rows)

    def backward_step(step_index, loop_state):
        query_grad, pair_all = loop_state
        key_block, value_block, place = gathered_block(step_index)
        grad_part, term_part = backward_block(
            query_rows,
            grad_rows,
            key_block,
            value_block,
            query_place,
            place,
            log_total,
            row_delta,
            softmax_scale,
        )
        pair_all = lax.dynamic_update_slice_in_dim(pair_all, term_part, step_index * step_rows, 0)
        return (query_grad + grad_part, pair_all)

    start_state = (
        jnp.zeros((row_count, group_size, head_size), jnp.float32),
        jnp.zeros((total_rows, 2 * head_size), jnp.float32),
    )
    query_grad, pair_all = lax.fori_loop(0, step_count, backward_step, start_state)
    pair_grad = sum_by_chip(pair_all, ("ctx_0", "ctx_1"), "ctx_2", 0)
    message = jnp.concatenate(
        [query_grad.reshape(row_count, group_size * head_size), pair_grad], axis=1
    ).astype(jnp.bfloat16)
    passed = passed_along(message, "section", -1)
    return passed[None]


def solution(mesh):
    split = Mesh(
        mesh.devices.reshape(mesh.shape["section"], 8, 4, 2), ("section", "ctx_0", "ctx_1", "ctx_2")
    )
    return jax.shard_map(
        per_device,
        mesh=split,
        in_specs=(
            P("section", None, CTX, None),
            P("section", None, CTX, None),
            P("section", None, CTX, None),
            P("section", CTX, None),
            P(CTX),
            P("section"),
        ),
        out_specs=P("section", CTX, None),
        check_vma=False,
    )
```

profile of v0, /device:TPU:24, one launch (start us, length us, event | category | flops | bytes accessed | tf_op | source)
XLA Modules:
  0.0 647.0 jit_solution(10081497542492428511)
XLA Ops:
  10.2 1.3 dynamic-slice.3
  13.0 26.4 %all-reduce = s32[128]{0:T(128)S(1)} all-reduce(s32[128]{0:T(128)S(1)} %dynamic-update-slice), channel_id=1, replica_groups=mesh['section'=16,'ctx_0'=8,'ctx_1'=4,'ctx_2'=2] {'ctx_0','ctx_1','ctx_2'}, use_global_device_ids=true, to_apply=%add | all-reduce | flops 128 | bytes 1024
  40.1 110.1 %all-gather.2.cloned.1.call-done = bf16[8192,256]{1,0:T(8,128)(2,1)} async-done(((bf16[128,256]{1,0:T(8,128)(2,1)}), bf16[8192,256]{1,0:T(8,128)(2,1)}) %all-gather.2.cloned.1.call-update) | async-done | bytes 4194320 | tf_op jit(solution)/shard_map/all_gather | solution.py:23
  150.2 4.5 fusion.50
  154.7 50.8 %while.40 = (s32[]{:T(128)}, f32[128,4]{0,1:T(4,128)S(1)}, f32[128,4]{0,1:T(4,128)S(1)}, f32[128,4,128]{2,0,1:T(8,128)S(1)}, s32[128]{0:T(128)S(1)}, /*index=5*/...) while((s32[]{:T(128)}, f32[128,4]{0,1:T(4,128)S(1)}, ...), condition=%wide.region_5.6_spmd.clone, body=%wide.region_1.5_spmd.clone.sunk | while | flops 136861696 | bytes 4371305 | solution.py:161
  156.5 1.3 convolution_add_fusion.4
  159.6 1.3 convolution_add_fusion.4
  162.8 1.3 convolution_add_fusion.4
  166.0 1.3 convolution_add_fusion.4
  169.2 1.3 convolution_add_fusion.4
  172.3 1.3 convolution_add_fusion.4
  175.5 1.3 convolution_add_fusion.4
  178.7 1.3 convolution_add_fusion.4
  181.9 1.3 convolution_add_fusion.4
  185.0 1.3 convolution_add_fusion.4
  188.2 1.3 convolution_add_fusion.4
  191.4 1.3 convolution_add_fusion.4
  194.6 1.3 convolution_add_fusion.4
  197.7 1.3 convolution_add_fusion.4
  200.9 1.3 convolution_add_fusion.4
  204.1 1.3 convolution_add_fusion.4
  205.7 4.2 broadcast_in_dim.217
  209.9 88.7 %while.41 = (s32[]{:T(128)}, f32[128,4,128]{2,0,1:T(8,128)S(1)}, f32[8192,256]{0,1:T(8,128)}, s32[128]{0:T(128)S(1)}, s32[128]{0:T(128)S(1)}, /*index=5*/bf16[81...) while((s32[]{:T(128)}, f32[128,4,128]{2,0,1:T(8,128)S(1)}, ...), condition=%wide.region_9.10_spmd.clone, body=%wide.region_7.9_spmd.clone.sunk | while | flops 337989120 | bytes 7881599 | solution.py:185
  210.2 1.2 fusion.94
  212.9 1.3 convolution_add_fusion.5
  218.5 1.3 convolution_add_fusion.5
  221.3 1.2 fusion.94
  224.1 1.3 convolution_add_fusion.5
  229.6 1.3 convolution_add_fusion.5
  235.2 1.3 convolution_add_fusion.5
  240.7 1.3 convolution_add_fusion.5
  246.2 1.3 convolution_add_fusion.5
  251.8 1.3 convolution_add_fusion.5
  257.3 1.3 convolution_add_fusion.5
  262.8 1.3 convolution_add_fusion.5
  268.4 1.3 convolution_add_fusion.5
  273.9 1.3 convolution_add_fusion.5
  279.5 1.3 convolution_add_fusion.5
  282.2 1.2 fusion.94
  285.0 1.3 convolution_add_fusion.5
  290.5 1.3 convolution_add_fusion.5
  296.1 1.3 convolution_add_fusion.5
  298.5 11.7 %reshape_reshape.3 = f32[32,2,128,256]{2,1,0,3:T(2,128)} reshape(f32[8192,256]{0,1:T(8,128)} %get-tuple-element.624) | data formatting | bytes 16777216 | tf_op jit(solution)/shard_map/reshape;reshape | solution.py:36
  310.2 13.4 %copy.30 = f32[32,2,128,256]{3,2,0,1:T(8,128)} copy(f32[32,2,128,256]{2,1,0,3:T(2,128)} %reshape_reshape.3) | data formatting | bytes 16777216 | tf_op jit(solution)/shard_map/reshape;reshape | solution.py:36
  323.7 32.7 %reduce-scatter.3.cloned.1.call-done = f32[32,128,256]{2,1,0:T(8,128)} async-done(((f32[64,128,256]{2,1,0:T(8,128)}), f32[32,128,256]{2,1,0:T(8,128)}) %reduce-scatter.3.cloned.1.call-update) | async-done | bytes 4194320 | tf_op jit(solution)/shard_map/reduce_scatter | solution.py:37
  356.5 265.5 %reduce-scatter.5.cloned.1.call-done = f32[1,128,256]{2,1,0:T(8,128)} async-done(((f32[32,128,256]{2,1,0:T(8,128)}), f32[1,128,256]{2,1,0:T(8,128)}) %reduce-scatter.5.cloned.1.call-update) | async-done | bytes 131088 | tf_op jit(solution)/shard_map/reduce_scatter | solution.py:38
  623.0 8.4 %collective-permute-start = (bf16[128,768]{1,0:T(8,128)(2,1)S(1)}, bf16[128,768]{1,0:T(8,128)(2,1)S(1)}, u32[]{:S(2)}, u32[]{:S(2)}) collective-permute-start(bf16[128,768]{1,0:T(8,128)(2,1)S(1)} %pad_maximum_fusion), channel_id=1, source_target_pairs={{0,960},{64,0},{128,64},{192,128},{256,192},{320,256},{384,320},{4... | collective-permute-start | bytes 589832 | tf_op jit(solution)/shard_map/ppermute | solution.py:44
  631.4 8.3 %collective-permute-done = bf16[128,768]{1,0:T(8,128)(2,1)S(1)} collective-permute-done((bf16[128,768]{1,0:T(8,128)(2,1)S(1)}, bf16[128,768]{1,0:T(8,128)(2,1)S(1)}, u32[]{:S(2)}, u32[]{:S(2)}) %collective-permute-start) | collective-permute-done | bytes 196640 | tf_op jit(solution)/shard_map/ppermute | solution.py:44
  (347 shorter events, 98.2 us)
Async XLA Ops:
  6.5 2.3 copy-start
  6.5 143.7 %all-gather.2.cloned.1.call-start = ((), (), s32[]{:S(2)}) async-start(), calls=%async_computation.2 | async-start | bytes 4259840 | tf_op jit(solution)/shard_map/all_gather | solution.py:23
  8.7 347.7 %reduce-scatter.3.cloned.1.call-start = ((), (), s32[]{:S(2)}) async-start(), calls=%async_computation.3 | async-start | bytes 12582912 | tf_op jit(solution)/shard_map/reduce_scatter | solution.py:37
  323.7 298.4 %reduce-scatter.5.cloned.1.call-start = ((), (), s32[]{:S(2)}) async-start(), calls=%async_computation.4 | async-start | bytes 4325376 | tf_op jit(solution)/shard_map/reduce_scatter | solution.py:38
  623.0 16.8 %collective-permute-start = (bf16[128,768]{1,0:T(8,128)(2,1)S(1)}, bf16[128,768]{1,0:T(8,128)(2,1)S(1)}, u32[]{:S(2)}, u32[]{:S(2)}) collective-permute-start(bf16[128,768]{1,0:T(8,128)(2,1)S(1)} %pad_maximum_fusion), channel_id=1, source_target_pairs={{0,960},{64,0},{128,64},{192,128},{256,192},{320,256},{384,320},{4... | collective-permute-start | bytes 589832 | tf_op jit(solution)/shard_map/ppermute | solution.py:44
Sparse Core Ops, SparseCore 0:
  10.1 140.0 all-gather.1
  323.8 32.6 reduce-scatter.2
  359.9 262.1 reduce-scatter.4
where the time goes:
time: 649 us; the launch traced here: 647 us
  waiting for transfers between devices  417 us (64%)
  matrix products  110 us (17%)
  local copies, waits for them, and re-layouts  41.3 us (6%)
  other arithmetic  27.2 us (4%)
  blocking collectives  26.4 us (4%)
  between operations  14.6 us (2%)
  starting transfers between devices  8.53 us (1%)
    reduce_scatter x1, waiting for transfers between devices, sum_by_chip(): return lax.psum_scatter(parts, chips, scatter_dimension=0, tiled=True)[0]  266 us
    all_gather x1, waiting for transfers between devices, sent_together(): lax.all_gather(both, axis, axis=dim, tiled=True)  110 us
    dot_general x32, matrix products, block_scores(): jnp.einsum('thd,cd->thc', query_rows, key_block, preferred_element_type=j...  39.5 us
    reduce_scatter x1, waiting for transfers between devices, sum_by_chip(): parts = lax.psum_scatter(parts, core, scatter_dimension=0, tiled=True)  32.7 us
    unnamed x1, blocking collectives  26.4 us
    another operation x2, local copies, waits for them, and re-layouts, sum_by_chip(): parts = parts.reshape(*sizes, *inside).swapaxes(0, 1).reshape(-1, *inside)  25.1 us
    dot_general x16, matrix products, forward_block(): jnp.einsum('thc,cd->thd', weights.astype(jnp.bfloat16), value_block, pref...  21.5 us
    dot_general x16, matrix products, backward_block(): jnp.einsum('thc,cd->thd', score_grad, key_block, preferred_element_type=j...  20.5 us
  transfers between devices with their start and end apart: 4, of which 4 were waited for; matrix products, arithmetic and copies ran while one was open for 1% of the time, Pallas kernels for 0%

commit v1 on v0

v1 whole, which is shorter than its diff:
```python
import functools
import math

import jax
import jax.numpy as jnp
from jax import lax
from jax.experimental import pallas as pl
from jax.experimental.pallas import tpu as pltpu
from jax.sharding import Mesh
from jax.sharding import PartitionSpec as P

Z, X, CORE, SECTION = "ctx_0", "ctx_1", "ctx_2", "section"
CTX = (Z, X, CORE)
MESH = pl.DeviceIdType.MESH
VMEM = pl.BlockSpec(memory_space=pltpu.VMEM)
SMEM = pl.BlockSpec(memory_space=pltpu.SMEM)
ANY = pl.BlockSpec(memory_space=pl.ANY)
DMA = pltpu.SemaphoreType.DMA
VMEM_LIMIT = 60 * 1024 * 1024

ID_ROWS = 16
masked_score = -1e30


def neighbours(nz, nx):
    z, x, core = lax.axis_index(Z), lax.axis_index(X), lax.axis_index(CORE)
    right = lax.rem(x + 1, nx)
    left = lax.rem(x + nx - 1, nx)
    far = lax.rem(x + nx // 2, nx)
    return z, x, core, right, left, far


def greet(nz, z, core, right, left, more=0):
    barrier = pltpu.get_barrier_semaphore()

    def signal(**where):
        pl.semaphore_signal(barrier, inc=1, device_id=dict(where), device_id_type=MESH)

    signal(**{X: right})
    signal(**{X: left})
    signal(**{CORE: 1 - core})

    @pl.when(z > 0)
    def _():
        signal(**{Z: z - 1})

    @pl.when(z < nz - 1)
    def _():
        signal(**{Z: z + 1})

    inside = (z > 0).astype(jnp.int32) + (z < nz - 1).astype(jnp.int32)
    pl.semaphore_wait(barrier, 3 + more + inside)


def remote(src, dst, send, recv, where):
    return pltpu.make_async_remote_copy(
        src_ref=src, dst_ref=dst, send_sem=send, recv_sem=recv, device_id=where, device_id_type=MESH
    )


def gather_kernel(nz, nx, blk, out, zs, zr, xs, xr, hs, hr, ps, pr, own_sem):
    z, x, core, right, left, far = neighbours(nz, nx)
    rows = blk.shape[0]
    cut = rows // 2 // 16 * 16
    halves = (pl.ds(0, cut), pl.ds(cut, rows - cut))

    def slot(zz, xx, cc):
        return (zz * nx + xx) * 2 + cc

    own = pltpu.make_async_copy(blk, out.at[slot(z, x, core)], own_sem)
    own.start()
    greet(nz, z, core, right, left)

    def along_z(src, zz, up):
        to = z + 1 if up else z - 1
        return remote(src, out.at[slot(zz, x, core)], zs.at[0 if up else 1, zz], zr.at[zz], {Z: to})

    def along_x(src, zz, xx, way):
        to = right if way == 0 else left
        return remote(src, out.at[slot(zz, xx, core)], xs.at[way, zz], xr.at[way, zz], {X: to})

    def half_on(zz, xx, way):
        to = right if way == 0 else left
        piece = out.at[slot(zz, xx, core), halves[way]]
        return remote(piece, piece, hs.at[way, zz], hr.at[way, zz], {X: to})

    def across(src, zz, xx):
        at = zz * nx + xx
        return remote(src, out.at[slot(zz, xx, core)], ps.at[at], pr.at[at], {CORE: 1 - core})

    def here(zz, xx):
        return out.at[slot(zz, xx, core)]

    def spread(src, zz):
        along_x(src, zz, x, 0).start()
        along_x(src, zz, x, 1).start()
        across(src, zz, x).start()

    @pl.when(z < nz - 1)
    def _():
        along_z(blk, z, True).start()

    @pl.when(z > 0)
    def _():
        along_z(blk, z, False).start()

    spread(blk, z)

    def z_stage(s):
        @pl.when(z - s >= 0)
        def _():
            zz = z - s
            along_z(here(zz, x), zz, True).wait_recv()

            @pl.when(z < nz - 1)
            def _():
                along_z(here(zz, x), zz, True).start()

            spread(here(zz, x), zz)

        @pl.when(z + s <= nz - 1)
        def _():
            zz = z + s
            along_z(here(zz, x), zz, False).wait_recv()

            @pl.when(z > 0)
            def _():
                along_z(here(zz, x), zz, False).start()

            spread(here(zz, x), zz)

    def x_one(zz):
        along_x(here(zz, left), zz, left, 0).wait_recv()
        half_on(zz, left, 0).start()
        across(here(zz, left), zz, left).start()
        along_x(here(zz, right), zz, right, 1).wait_recv()
        half_on(zz, right, 1).start()
        across(here(zz, right), zz, right).start()

    def h_one(zz):
        half_on(zz, far, 0).wait_recv()
        half_on(zz, far, 1).wait_recv()
        across(here(zz, far), zz, far).start()

    def both_ways(one, t):
        @pl.when(z - t >= 0)
        def _():
            one(z - t)

        @pl.when((t > 0) & (z + t <= nz - 1))
        def _():
            one(z + t)

    def step(s, _):
        @pl.when(s < nz)
        def _():
            z_stage(s)

        @pl.when(s <= nz)
        def _():
            both_ways(x_one, s - 1)

        @pl.when(s >= 2)
        def _():
            both_ways(h_one, s - 2)

        return 0

    lax.fori_loop(1, nz + 2, step, 0)

    def drain(zz, _):
        @pl.when((zz <= z) & (z < nz - 1))
        def _():
            along_z(here(zz, x), zz, True).wait_send()

        @pl.when((zz >= z) & (z > 0))
        def _():
            along_z(here(zz, x), zz, False).wait_send()

        for way in (0, 1):
            along_x(here(zz, x), zz, x, way).wait_send()
            half_on(zz, left if way == 0 else right, way).wait_send()
        for xx in range(nx):
            across(here(zz, xx), zz, xx).wait_send()
            at = zz * nx + xx
            other = out.at[slot(zz, xx, 1 - core)]
            remote(other, other, ps.at[at], pr.at[at], {CORE: 1 - core}).wait_recv()
        return 0

    lax.fori_loop(0, nz, drain, 0)
    own.wait()


def gathered(blk, nz, nx):
    shape = (nz * nx * 2, *blk.shape)
    return pl.pallas_call(
        functools.partial(gather_kernel, nz, nx),
        out_shape=jax.ShapeDtypeStruct(shape, blk.dtype),
        in_specs=[VMEM],
        out_specs=VMEM,
        scratch_shapes=[
            DMA((2, nz)),
            DMA((nz,)),
            DMA((2, nz)),
            DMA((2, nz)),
            DMA((2, nz)),
            DMA((2, nz)),
            DMA((nz * nx,)),
            DMA((nz * nx,)),
            DMA,
        ],
        compiler_params=pltpu.CompilerParams(
            collective_id=0, has_side_effects=True, vmem_limit_bytes=VMEM_LIMIT
        ),
        name="gather",
    )(blk)


def attend_kernel(
    group,
    head,
    half,
    scale,
    stash,
    ids,
    own_ids,
    queries,
    grads,
    blocks,
    dq,
    dkv,
    q_full,
    qs,
    gs,
    tops,
    totals,
    deltas,
    dq_sum,
    scores,
    dprobs,
    where_is,
    sem,
):
    total = ids.shape[0]
    per = 256 // half
    tiles = total // per
    rows = group * half
    fetch = pltpu.make_async_copy(queries.at[0, stash[0]], q_full, sem)
    fetch.start()

    def place(i, _):
        where_is[ids[i]] = i
        return 0

    lax.fori_loop(0, total, place, 0)
    low_first = (own_ids[0] < own_ids[1]).astype(jnp.int32)
    low = jnp.minimum(own_ids[0], own_ids[1])
    high = total - 1 - low
    halves = (low_first * half, (1 - low_first) * half)
    fetch.wait()
    for p in (0, 1):
        base = pl.multiple_of(halves[p], half)
        for h in range(group):
            cols = slice(h * head, (h + 1) * head)
            qs[p, h * half : (h + 1) * half, :] = q_full[pl.ds(base, half), cols]
            gs[p, h * half : (h + 1) * half, :] = grads[0, pl.ds(base, half), cols]
    tops[...] = jnp.full_like(tops, masked_score)
    totals[...] = jnp.zeros_like(totals)
    deltas[...] = jnp.zeros_like(deltas)
    dq_sum[...] = jnp.zeros_like(dq_sum)

    high_tiles = high // per + 1
    exp_scale = scale * math.log2(math.e)
    gap = lax.broadcasted_iota(jnp.int32, (256, rows), 0) - (
        lax.broadcasted_iota(jnp.int32, (256, rows), 1) % half
    )

    def unit(u):
        p = (u >= high_tiles).astype(jnp.int32)
        return p, u - p * high_tiles

    def tile_of(tile, first):
        pieces = []
        for i in range(per):
            at = where_is[tile * per + i]
            start = pl.multiple_of(first + (at % 2) * half, half)
            pieces.append(blocks[at // 2, pl.ds(start, half), :])
        return jnp.concatenate(pieces, axis=0)

    def cross(a, b, dims):
        return lax.dot_general(a, b, (dims, ((), ())), preferred_element_type=jnp.float32)

    def forward(u):
        p, tile = unit(u)
        mine = jnp.where(p == 0, high, low)
        t = cross(tile_of(tile, 0), qs[p], ((1,), (1,))) * exp_scale
        t = jnp.where(gap <= mine * half - tile * 256, t, masked_score)
        dprob = cross(tile_of(tile, 2 * half), gs[p], ((1,), (1,)))
        scores[u] = t
        dprobs[u] = dprob
        old = tops[p]
        new = jnp.maximum(old, jnp.max(t, axis=0, keepdims=True))
        fading = jnp.exp2(old - new)
        e = jnp.exp2(t - new)
        tops[p] = new
        totals[p] = totals[p] * fading + jnp.sum(e, axis=0, keepdims=True)
        deltas[p] = deltas[p] * fading + jnp.sum(e * dprob, axis=0, keepdims=True)

    units = tiles + 1
    together = 3 if units % 3 == 0 else 1

    def forward_step(i, _):
        for k in range(together):
            forward(i * together + k)
        return 0

    lax.fori_loop(0, units // together, forward_step, 0)
    deltas[...] = deltas[...] / totals[...]
    tops[...] = tops[...] + jnp.log2(totals[...])

    def backward(u):
        p, tile = unit(u)
        weights = jnp.exp2(scores[u] - tops[p])
        probs = weights.astype(jnp.bfloat16)
        dscore = (weights * (dprobs[u] - deltas[p]) * scale).astype(jnp.bfloat16)
        dk = cross(dscore, qs[p], ((1,), (0,)))
        dv = cross(probs, gs[p], ((1,), (0,)))
        dq_sum[p] += cross(tile_of(tile, 0), dscore, ((0,), (0,)))
        for i in range(per):
            at = where_is[tile * per + i]
            here = slice(i * half, (i + 1) * half)
            for part, first in ((dk, 0), (dv, 2 * half)):
                spot = (at // 2, pl.ds(pl.multiple_of(first + (at % 2) * half, half), half))
                before = jnp.where(p == 1, dkv[spot].astype(jnp.float32), 0.0)
                dkv[spot] = (before + part[here]).astype(jnp.bfloat16)

    def backward_step(i, _):
        for k in range(together):
            backward(i * together + k)
        return 0

    lax.fori_loop(0, units // together, backward_step, 0)

    def clear(s, _):
        at = where_is[s]
        for first in (0, 2 * half):
            spot = (at // 2, pl.ds(pl.multiple_of(first + (at % 2) * half, half), half))
            dkv[spot] = jnp.zeros((half, head), jnp.bfloat16)
        return 0

    lax.fori_loop(high_tiles * per, total, clear, 0)
    for p in (0, 1):
        base = pl.multiple_of(halves[p], half)
        turned = dq_sum[p].T.astype(jnp.bfloat16)
        for h in range(group):
            dq[pl.ds(base, half), h * head : (h + 1) * head] = turned[h * half : (h + 1) * half]


def attended(stash, ids, own_ids, queries, grads, blocks, head):
    tokens, width = queries.shape[2:]
    group, half = width // head, tokens // 2
    rows = group * half
    units = ids.shape[0] * half // 256 + 1
    return pl.pallas_call(
        functools.partial(attend_kernel, group, head, half, 1.0 / math.sqrt(head)),
        out_shape=(
            jax.ShapeDtypeStruct((tokens, width), jnp.bfloat16),
            jax.ShapeDtypeStruct((blocks.shape[0], 2 * tokens, head), jnp.bfloat16),
        ),
        in_specs=[SMEM, SMEM, SMEM, ANY, VMEM, VMEM],
        out_specs=(VMEM, VMEM),
        scratch_shapes=[
            pltpu.VMEM((tokens, width), jnp.bfloat16),
            pltpu.VMEM((2, rows, head), jnp.bfloat16),
            pltpu.VMEM((2, rows, head), jnp.bfloat16),
            pltpu.VMEM((2, 1, rows), jnp.float32),
            pltpu.VMEM((2, 1, rows), jnp.float32),
            pltpu.VMEM((2, 1, rows), jnp.float32),
            pltpu.VMEM((2, head, rows), jnp.float32),
            pltpu.VMEM((units, 256, rows), jnp.float32),
            pltpu.VMEM((units, 256, rows), jnp.float32),
            pltpu.SMEM((ids.shape[0],), jnp.int32),
            DMA,
        ],
        compiler_params=pltpu.CompilerParams(vmem_limit_bytes=VMEM_LIMIT),
        name="attend",
    )(stash, ids, own_ids, queries, grads, blocks)


def scatter_kernel(
    nz, nx, ns, dq, dkv, out, rx, held, hbuf, xbuf, zbuf, last, ps, pr, hs, hr, xs, xr, zs, zr, ms, mr
):
    z, x, core, right, left, far = neighbours(nz, nx)
    section = lax.axis_index(SECTION)
    ahead = lax.rem(section + ns - 1, ns)
    behind = lax.rem(section + 1, ns)
    tokens, width = dq.shape
    head = dkv.shape[2]
    ways = (right, left)

    barrier = pltpu.get_barrier_semaphore()
    pl.semaphore_signal(barrier, inc=1, device_id={SECTION: behind}, device_id_type=MESH)
    greet(nz, z, core, right, left, more=1)

    def pair(zz, xx):
        at = zz * nx + xx
        src = dkv.at[at * 2 + 1 - core]
        return remote(src, rx.at[at], ps.at[at], pr.at[at], {CORE: 1 - core})

    def nth(k):
        return jnp.where(k % 2 == 0, k // 2, nz - 1 - k // 2)

    main = remote(dq, out.at[:, pl.ds(0, width)], ms.at[0], mr.at[0], {SECTION: ahead})

    def launch(k, _):
        for xx in range(nx):
            pair(nth(k), xx).start()
        return 0

    lax.fori_loop(0, nz, launch, 0)
    main.start()

    def mine(zz, xx):
        at = zz * nx + xx
        return dkv[at * 2 + core].astype(jnp.float32) + rx[at].astype(jnp.float32)

    def half_on(zz, way):
        piece = held.at[zz, 0, pl.ds(way * tokens, tokens)]
        return remote(piece, hbuf.at[way, zz], hs.at[way, zz], hr.at[way, zz], {X: ways[way]})

    def along_x(zz, way):
        return remote(
            held.at[zz, 1 + way], xbuf.at[way, zz], xs.at[way, zz], xr.at[way, zz], {X: ways[way]}
        )

    def first(zz):
        for xx in range(nx):
            pair(zz, xx).wait_recv()
        held[zz, 0] = mine(zz, far).astype(jnp.bfloat16)
        half_on(zz, 0).start()
        half_on(zz, 1).start()

    def second(zz):
        for way in (0, 1):
            half_on(zz, way).wait_recv()
            own = mine(zz, ways[way])
            more = hbuf[way, zz].astype(jnp.float32)
            keep = (1 - way) * tokens
            joined = own[way * tokens : (way + 1) * tokens] + more
            held[zz, 1 + way, way * tokens : (way + 1) * tokens] = joined.astype(jnp.bfloat16)
            held[zz, 1 + way, keep : keep + tokens] = own[keep : keep + tokens].astype(jnp.bfloat16)
            along_x(zz, way).start()

    def third(zz):
        along_x(zz, 0).wait_recv()
        along_x(zz, 1).wait_recv()
        done = mine(zz, x) + xbuf[0, zz].astype(jnp.float32) + xbuf[1, zz].astype(jnp.float32)
        held[zz, 3] = done.astype(jnp.bfloat16)

    def step(k, _):
        @pl.when(k < nz)
        def _():
            first(nth(k))

        @pl.when((k >= 1) & (k <= nz))
        def _():
            second(nth(k - 1))

        @pl.when(k >= 2)
        def _():
            third(nth(k - 2))

        return 0

    lax.fori_loop(0, nz + 2, step, 0)

    pieces = (pl.ds(0, tokens), pl.ds(tokens, tokens))

    def along_z(zz, down, piece):
        to = z - 1 if down else z + 1
        way = 0 if down else 1
        return remote(
            held.at[zz, 3, pieces[piece]],
            zbuf.at[way, zz, pieces[piece]],
            zs.at[way, zz, piece],
            zr.at[way, zz, piece],
            {Z: to},
        )

    def chain(zz, down, source):
        way = 0 if down else 1
        for piece in (0, 1):

            @pl.when(source)
            def _():
                along_z(zz, down, piece).wait_recv()
                joined = held[zz, 3, pieces[piece]].astype(jnp.float32) + zbuf[
                    way, zz, pieces[piece]
                ].astype(jnp.float32)
                held[zz, 3, pieces[piece]] = joined.astype(jnp.bfloat16)

            along_z(zz, down, piece).start()

    def chains(i, _):
        @pl.when(i < z)
        def _():
            chain(i, True, z < nz - 1)

        @pl.when(nz - 1 - i > z)
        def _():
            chain(nz - 1 - i, False, z > 0)

        return 0

    lax.fori_loop(0, nz - 1, chains, 0)

    for piece in (0, 1):
        last[pieces[piece]] = held[z, 3, pieces[piece]].astype(jnp.float32)

        @pl.when(z < nz - 1)
        def _():
            along_z(z, True, piece).wait_recv()
            last[pieces[piece]] += zbuf[0, z, pieces[piece]].astype(jnp.float32)

        @pl.when(z > 0)
        def _():
            along_z(z, False, piece).wait_recv()
            last[pieces[piece]] += zbuf[1, z, pieces[piece]].astype(jnp.float32)

        held[z, 3, pieces[piece]] = last[pieces[piece]].astype(jnp.bfloat16)

    def tail(piece):
        return remote(
            held.at[z, 3, pieces[piece]],
            out.at[:, pl.ds(width + piece * head, head)],
            ms.at[1 + piece],
            mr.at[1 + piece],
            {SECTION: ahead},
        )

    for piece in (0, 1):
        tail(piece).start()

    def drain(zz, _):
        for xx in range(nx):
            pair(zz, xx).wait_send()
        for way in (0, 1):
            half_on(zz, way).wait_send()
            along_x(zz, way).wait_send()
        for piece in (0, 1):

            @pl.when(zz < z)
            def _():
                along_z(zz, True, piece).wait_send()

            @pl.when(zz > z)
            def _():
                along_z(zz, False, piece).wait_send()

        return 0

    lax.fori_loop(0, nz, drain, 0)
    main.wait()
    for piece in (0, 1):
        tail(piece).wait()


def scattered(dq, dkv, nz, nx, ns):
    tokens, width = dq.shape
    rows, head = dkv.shape[1:]
    half = jnp.bfloat16
    return pl.pallas_call(
        functools.partial(scatter_kernel, nz, nx, ns),
        out_shape=jax.ShapeDtypeStruct((tokens, width + 2 * head), half),
        in_specs=[VMEM, VMEM],
        out_specs=VMEM,
        scratch_shapes=[
            pltpu.VMEM((nz * nx, rows, head), half),
            pltpu.VMEM((nz, 4, rows, head), half),
            pltpu.VMEM((2, nz, rows // 2, head), half),
            pltpu.VMEM((2, nz, rows, head), half),
            pltpu.VMEM((2, nz, rows, head), half),
            pltpu.VMEM((rows, head), jnp.float32),
            DMA((nz * nx,)),
            DMA((nz * nx,)),
            DMA((2, nz)),
            DMA((2, nz)),
            DMA((2, nz)),
            DMA((2, nz)),
            DMA((2, nz, 2)),
            DMA((2, nz, 2)),
            DMA((3,)),
            DMA((3,)),
        ],
        compiler_params=pltpu.CompilerParams(
            collective_id=1, has_side_effects=True, vmem_limit_bytes=VMEM_LIMIT
        ),
        name="scatter",
    )(dq, dkv)


def per_device(sizes, queries, keys, values, out_grad, stretch_ids, stash_slot):
    ns, nz, nx = sizes
    stash_index = stash_slot[0]
    key_rows = lax.dynamic_index_in_dim(keys[0], stash_index, 0, keepdims=False)
    value_rows = lax.dynamic_index_in_dim(values[0], stash_index, 0, keepdims=False)
    head = key_rows.shape[1]
    lane = lax.broadcasted_iota(jnp.int32, (ID_ROWS, head), 1)
    id_rows = jnp.where(lane < head // 2, stretch_ids[0], stretch_ids[1]).astype(jnp.bfloat16)
    blk = jnp.concatenate([key_rows, value_rows, id_rows], axis=0)
    blocks = gathered(blk, nz, nx)
    ids = blocks[:, 2 * key_rows.shape[0], :: head // 2].astype(jnp.int32).reshape(-1)
    dq, dkv = attended(stash_slot, ids, stretch_ids, queries, out_grad, blocks, head)
    return scattered(dq, dkv, nz, nx, ns)[None]


def solution(mesh):
    ns = mesh.shape["section"]
    nz, nx = 8, 4
    split = Mesh(mesh.devices.reshape(ns, nz, nx, 2), (SECTION, Z, X, CORE))
    return jax.shard_map(
        functools.partial(per_device, (ns, nz, nx)),
        mesh=split,
        in_specs=(
            P(SECTION, None, CTX, None),
            P(SECTION, None, CTX, None),
            P(SECTION, None, CTX, None),
            P(SECTION, CTX, None),
            P(CTX),
            P(SECTION),
        ),
        out_specs=P(SECTION, CTX, None),
        check_vma=False,
    )
```

time: 649 us -> 197 us (0.30)
  the two profiles are of different devices: /device:TPU:24 before, /device:TPU:98 now
where the time goes in v1:
time: 197 us; the launch traced here: 196 us
  Pallas kernels  187 us (95%)
  local copies, waits for them, and re-layouts  6.2 us (3%)
    pallas_call x1, Pallas kernels, scattered(): pl.pallas_call(functools.partial(scatter_kernel, nz, nx, ns), out_shape=j...  132 us
    pallas_call x1, Pallas kernels, gathered(): pl.pallas_call(functools.partial(gather_kernel, nz, nx), out_shape=jax.Sh...  37.6 us
    pallas_call x1, Pallas kernels, attended(): pl.pallas_call(functools.partial(attend_kernel, group, head, half, 1.0 /...  16.7 us

profile of v1, /device:TPU:98, one launch (start us, length us, event | category | flops | bytes accessed | tf_op | source)
XLA Modules:
  0.0 195.5 jit_solution(8325408529417236869)
XLA Ops:
  0.7 1.3 fusion.1
  2.0 1.2 fusion
  3.2 0.8 dynamic-slice_bitcast_fusion
  4.0 0.6 pad_maximum_fusion.blk
  4.6 37.6 %gather.1.blocks = bf16[64,272,128]{2,1,0:T(8,128)(2,1)} custom-call(bf16[272,128]{1,0:T(8,128)(2,1)} %pad_maximum_fusion.blk), custom_call_target="tpu_custom_call" | custom-call | tf_op jit(solution)/shard_map/gather/pallas_call | solution.py:196
  42.2 1.8 slice.11
  44.1 0.1 convert_reduce_fusion
  44.2 0.7 reshape.8.ids
  44.9 16.7 %attend.1 = (bf16[128,512]{1,0:T(8,128)(2,1)}, bf16[64,256,128]{2,1,0:T(8,128)(2,1)}) custom-call(s32[1]{0:T(128)} %copy.8.stash, s32[128]{0:T(128)} %reshape.8.ids, s32[2]{0:T(128)} %own_ids.1, bf16[1,8,128,512]{3,2,1,0:T(8,128)(2,1)} %queries.1, bf16[1,128,512]{2,1,0:T(8,128)(2,1)} %grads.1, bf16[64,272,128]{2,1,0:T(8,128)(2,1)} %gather.1.blocks), custom_call_target="tpu_custom_call" | custom-call | tf_op jit(solution)/shard_map/attend/pallas_call | solution.py:364
  61.6 132.3 %scatter.1 = bf16[128,768]{1,0:T(8,128)(2,1)} custom-call(bf16[128,512]{1,0:T(8,128)(2,1)} %get-tuple-element.7.dq, bf16[64,256,128]{2,1,0:T(8,128)(2,1)} %get-tuple-element.8.dkv), custom_call_target="tpu_custom_call" | custom-call | tf_op jit(solution)/shard_map/scatter/pallas_call | solution.py:572
  193.9 1.6 copy.9
  (1 shorter events, 0.0 us)

commit v2 on v1

--- a/solution.py
+++ b/solution.py
@@ -457,23 +457,6 @@
         done = mine(zz, x) + xbuf[0, zz].astype(jnp.float32) + xbuf[1, zz].astype(jnp.float32)
         held[zz, 3] = done.astype(jnp.bfloat16)
 
-    def step(k, _):
-        @pl.when(k < nz)
-        def _():
-            first(nth(k))
-
-        @pl.when((k >= 1) & (k <= nz))
-        def _():
-            second(nth(k - 1))
-
-        @pl.when(k >= 2)
-        def _():
-            third(nth(k - 2))
-
-        return 0
-
-    lax.fori_loop(0, nz + 2, step, 0)
-
     pieces = (pl.ds(0, tokens), pl.ds(tokens, tokens))
 
     def along_z(zz, down, piece):
@@ -501,18 +484,42 @@
 
             along_z(zz, down, piece).start()
 
-    def chains(i, _):
-        @pl.when(i < z)
+    def up_chain(t):
+        i = t - z
+
+        @pl.when((i >= 0) & (i < nz - 1 - z))
+        def _():
+            chain(nz - 1 - i, False, z > 0)
+
+    def down_chain(t):
+        i = t - (nz - 1 - z)
+
+        @pl.when((i >= 0) & (i < z))
         def _():
             chain(i, True, z < nz - 1)
 
-        @pl.when(nz - 1 - i > z)
-        def _():
-            chain(nz - 1 - i, False, z > 0)
-
-        return 0
-
-    lax.fori_loop(0, nz - 1, chains, 0)
+    def step(k, _):
+        @pl.when(k < nz)
+        def _():
+            first(nth(k))
+
+        @pl.when((k >= 1) & (k <= nz))
+        def _():
+            second(nth(k - 1))
+
+        @pl.when((k >= 2) & (k <= nz + 1))
+        def _():
+            third(nth(k - 2))
+
+        @pl.when((k >= 3) & ((k % 2 == 1) | (k > nz + 1)))
+        def _():
+            t = jnp.where(k > nz + 1, k - (nz + 2) + nz // 2, (k - 3) // 2)
+            up_chain(t)
+            down_chain(t)
+
+        return 0
+
+    lax.fori_loop(0, nz + 2 + nz - 1 - nz // 2, step, 0)
 
     for piece in (0, 1):
         last[pieces[piece]] = held[z, 3, pieces[piece]].astype(jnp.float32)

time: 197 us -> 146 us (0.74)
  the two profiles are of different devices: /device:TPU:98 before, /device:TPU:58 now
where the time goes in v2:
time: 146 us
  Pallas kernels  137 us (94%)
  local copies, waits for them, and re-layouts  6.2 us (4%)
  other arithmetic  1.96 us (1%)
    pallas_call x1, Pallas kernels, scattered(): pl.pallas_call(functools.partial(scatter_kernel, nz, nx, ns), out_shape=j...  79.5 us
    pallas_call x1, Pallas kernels, gathered(): pl.pallas_call(functools.partial(gather_kernel, nz, nx), out_shape=jax.Sh...  40.7 us
    pallas_call x1, Pallas kernels, attended(): pl.pallas_call(functools.partial(attend_kernel, group, head, half, 1.0 /...  16.7 us

profile of v2, /device:TPU:58, one launch (start us, length us, event | category | flops | bytes accessed | tf_op | source)
XLA Modules:
  0.0 145.7 jit_solution(1856935900197303442)
XLA Ops:
  0.7 1.3 fusion.1
  2.0 1.2 fusion
  3.2 0.8 dynamic-slice_bitcast_fusion
  4.0 0.6 pad_maximum_fusion.blk
  4.6 40.7 %gather.1.blocks = bf16[64,272,128]{2,1,0:T(8,128)(2,1)} custom-call(bf16[272,128]{1,0:T(8,128)(2,1)} %pad_maximum_fusion.blk), custom_call_target="tpu_custom_call" | custom-call | tf_op jit(solution)/shard_map/gather/pallas_call | solution.py:196
  45.3 1.8 %slice.11 = bf16[64,1,2]{2,1,0:T(2,128)(2,1)S(1)} slice(bf16[64,272,128]{2,1,0:T(8,128)(2,1)} %gather.1.blocks), slice={[0:64:1], [256:257:1], [0:128:64]} | slice | bytes 512 | tf_op jit(solution)/shard_map/slice | solution.py:619
  47.2 0.1 convert_reduce_fusion
  47.3 0.7 reshape.8.ids
  47.9 16.7 %attend.1 = (bf16[128,512]{1,0:T(8,128)(2,1)}, bf16[64,256,128]{2,1,0:T(8,128)(2,1)}) custom-call(s32[1]{0:T(128)} %copy.8.stash, s32[128]{0:T(128)} %reshape.8.ids, s32[2]{0:T(128)} %own_ids.1, bf16[1,8,128,512]{3,2,1,0:T(8,128)(2,1)} %queries.1, bf16[1,128,512]{2,1,0:T(8,128)(2,1)} %grads.1, bf16[64,272,128]{2,1,0:T(8,128)(2,1)} %gather.1.blocks), custom_call_target="tpu_custom_call" | custom-call | tf_op jit(solution)/shard_map/attend/pallas_call | solution.py:364
  64.6 79.5 %scatter.1 = bf16[128,768]{1,0:T(8,128)(2,1)} custom-call(bf16[128,512]{1,0:T(8,128)(2,1)} %get-tuple-element.7.dq, bf16[64,256,128]{2,1,0:T(8,128)(2,1)} %get-tuple-element.8.dkv), custom_call_target="tpu_custom_call" | custom-call | tf_op jit(solution)/shard_map/scatter/pallas_call | solution.py:579
  144.1 1.6 %copy.9 = bf16[1,128,768]{2,1,0:T(8,128)(2,1)} copy(bf16[1,128,768]{2,1,0:T(8,128)(2,1)} %bitcast.11) | data formatting | bytes 393216
  (1 shorter events, 0.0 us)

commit v3 on v2

--- a/solution.py
+++ b/solution.py
@@ -15,10 +15,12 @@
 VMEM = pl.BlockSpec(memory_space=pltpu.VMEM)
 SMEM = pl.BlockSpec(memory_space=pltpu.SMEM)
 ANY = pl.BlockSpec(memory_space=pl.ANY)
+IN_HBM = pl.BlockSpec(memory_space=pltpu.HBM)
 DMA = pltpu.SemaphoreType.DMA
 VMEM_LIMIT = 60 * 1024 * 1024
 
 ID_ROWS = 16
+PIECES = 2
 masked_score = -1e30
 
 
@@ -63,6 +65,8 @@
     rows = blk.shape[0]
     cut = rows // 2 // 16 * 16
     halves = (pl.ds(0, cut), pl.ds(cut, rows - cut))
+    size = rows // PIECES // 16 * 16
+    pieces = [pl.ds(i * size, size if i < PIECES - 1 else rows - i * size) for i in range(PIECES)]
 
     def slot(zz, xx, cc):
         return (zz * nx + xx) * 2 + cc
@@ -71,9 +75,15 @@
     own.start()
     greet(nz, z, core, right, left)
 
-    def along_z(src, zz, up):
+    def along_z(src, zz, up, i):
         to = z + 1 if up else z - 1
-        return remote(src, out.at[slot(zz, x, core)], zs.at[0 if up else 1, zz], zr.at[zz], {Z: to})
+        return remote(
+            src.at[pieces[i]],
+            out.at[slot(zz, x, core), pieces[i]],
+            zs.at[0 if up else 1, zz, i],
+            zr.at[zz, i],
+            {Z: to},
+        )
 
     def along_x(src, zz, xx, way):
         to = right if way == 0 else left
@@ -98,11 +108,13 @@
 
     @pl.when(z < nz - 1)
     def _():
-        along_z(blk, z, True).start()
+        for i in range(PIECES):
+            along_z(blk, z, True, i).start()
 
     @pl.when(z > 0)
     def _():
-        along_z(blk, z, False).start()
+        for i in range(PIECES):
+            along_z(blk, z, False, i).start()
 
     spread(blk, z)
 
@@ -110,22 +122,24 @@
         @pl.when(z - s >= 0)
         def _():
             zz = z - s
-            along_z(here(zz, x), zz, True).wait_recv()
-
-            @pl.when(z < nz - 1)
-            def _():
-                along_z(here(zz, x), zz, True).start()
+            for i in range(PIECES):
+                along_z(here(zz, x), zz, True, i).wait_recv()
+
+                @pl.when(z < nz - 1)
+                def _():
+                    along_z(here(zz, x), zz, True, i).start()
 
             spread(here(zz, x), zz)
 
         @pl.when(z + s <= nz - 1)
         def _():
             zz = z + s
-            along_z(here(zz, x), zz, False).wait_recv()
-
-            @pl.when(z > 0)
-            def _():
-                along_z(here(zz, x), zz, False).start()
+            for i in range(PIECES):
+                along_z(here(zz, x), zz, False, i).wait_recv()
+
+                @pl.when(z > 0)
+                def _():
+                    along_z(here(zz, x), zz, False, i).start()
 
             spread(here(zz, x), zz)
 
@@ -171,11 +185,13 @@
     def drain(zz, _):
         @pl.when((zz <= z) & (z < nz - 1))
         def _():
-            along_z(here(zz, x), zz, True).wait_send()
+            for i in range(PIECES):
+                along_z(here(zz, x), zz, True, i).wait_send()
 
         @pl.when((zz >= z) & (z > 0))
         def _():
-            along_z(here(zz, x), zz, False).wait_send()
+            for i in range(PIECES):
+                along_z(here(zz, x), zz, False, i).wait_send()
 
         for way in (0, 1):
             along_x(here(zz, x), zz, x, way).wait_send()
@@ -199,8 +215,8 @@
         in_specs=[VMEM],
         out_specs=VMEM,
         scratch_shapes=[
-            DMA((2, nz)),
-            DMA((nz,)),
+            DMA((2, nz, PIECES)),
+            DMA((nz, PIECES)),
             DMA((2, nz)),
             DMA((2, nz)),
             DMA((2, nz)),
@@ -210,7 +226,7 @@
             DMA,
         ],
         compiler_params=pltpu.CompilerParams(
-            collective_id=0, has_side_effects=True, vmem_limit_bytes=VMEM_LIMIT
+            collective_id=0, has_side_effects=True, vmem_limit_bytes=8 * 1024 * 1024
         ),
         name="gather",
     )(blk)
@@ -222,7 +238,6 @@
     half,
     scale,
     stash,
-    ids,
     own_ids,
     queries,
     grads,
@@ -239,20 +254,21 @@
     scores,
     dprobs,
     where_is,
-    sem,
+    id_rows,
+    ids,
+    sems,
 ):
-    total = ids.shape[0]
+    total = 2 * blocks.shape[0]
     per = 256 // half
     tiles = total // per
     rows = group * half
-    fetch = pltpu.make_async_copy(queries.at[0, stash[0]], q_full, sem)
+    fetch = pltpu.make_async_copy(queries.at[0, stash[0]], q_full, sems.at[0])
     fetch.start()
 
-    def place(i, _):
-        where_is[ids[i]] = i
-        return 0
-
-    lax.fori_loop(0, total, place, 0)
+    numbers = blocks[:, 4 * half :, :].astype(jnp.float32)
+    id_rows[...] = jnp.max(numbers, axis=1).astype(jnp.int32)
+    listing = pltpu.make_async_copy(id_rows, ids, sems.at[1])
+    listing.start()
     low_first = (own_ids[0] < own_ids[1]).astype(jnp.int32)
     low = jnp.minimum(own_ids[0], own_ids[1])
     high = total - 1 - low
@@ -269,6 +285,14 @@
     deltas[...] = jnp.zeros_like(deltas)
     dq_sum[...] = jnp.zeros_like(dq_sum)
 
+    listing.wait()
+
+    def place(i, _):
+        where_is[ids[i, 0]] = 2 * i
+        where_is[ids[i, head // 2]] = 2 * i + 1
+        return 0
+
+    lax.fori_loop(0, total // 2, place, 0)
     high_tiles = high // per + 1
     exp_scale = scale * math.log2(math.e)
     gap = lax.broadcasted_iota(jnp.int32, (256, rows), 0) - (
@@ -356,18 +380,19 @@
             dq[pl.ds(base, half), h * head : (h + 1) * head] = turned[h * half : (h + 1) * half]
 
 
-def attended(stash, ids, own_ids, queries, grads, blocks, head):
+def attended(stash, own_ids, queries, grads, blocks, head):
     tokens, width = queries.shape[2:]
     group, half = width // head, tokens // 2
     rows = group * half
-    units = ids.shape[0] * half // 256 + 1
+    total = 2 * blocks.shape[0]
+    units = total * half // 256 + 1
     return pl.pallas_call(
         functools.partial(attend_kernel, group, head, half, 1.0 / math.sqrt(head)),
         out_shape=(
             jax.ShapeDtypeStruct((tokens, width), jnp.bfloat16),
             jax.ShapeDtypeStruct((blocks.shape[0], 2 * tokens, head), jnp.bfloat16),
         ),
-        in_specs=[SMEM, SMEM, SMEM, ANY, VMEM, VMEM],
+        in_specs=[SMEM, SMEM, ANY, VMEM, VMEM],
         out_specs=(VMEM, VMEM),
         scratch_shapes=[
             pltpu.VMEM((tokens, width), jnp.bfloat16),
@@ -379,12 +404,14 @@
             pltpu.VMEM((2, head, rows), jnp.float32),
             pltpu.VMEM((units, 256, rows), jnp.float32),
             pltpu.VMEM((units, 256, rows), jnp.float32),
-            pltpu.SMEM((ids.shape[0],), jnp.int32),
-            DMA,
+            pltpu.SMEM((total,), jnp.int32),
+            pltpu.VMEM((total // 2, head), jnp.int32),
+            pltpu.SMEM((total // 2, head), jnp.int32),
+            DMA((2,)),
         ],
-        compiler_params=pltpu.CompilerParams(vmem_limit_bytes=VMEM_LIMIT),
+        compiler_params=pltpu.CompilerParams(vmem_limit_bytes=32 * 1024 * 1024),
         name="attend",
-    )(stash, ids, own_ids, queries, grads, blocks)
+    )(stash, own_ids, queries, grads, blocks)
 
 
 def scatter_kernel(
@@ -412,13 +439,14 @@
 
     main = remote(dq, out.at[:, pl.ds(0, width)], ms.at[0], mr.at[0], {SECTION: ahead})
 
+    main.start()
+
     def launch(k, _):
         for xx in range(nx):
             pair(nth(k), xx).start()
         return 0
 
     lax.fori_loop(0, nz, launch, 0)
-    main.start()
 
     def mine(zz, xx):
         at = zz * nx + xx
@@ -521,21 +549,6 @@
 
     lax.fori_loop(0, nz + 2 + nz - 1 - nz // 2, step, 0)
 
-    for piece in (0, 1):
-        last[pieces[piece]] = held[z, 3, pieces[piece]].astype(jnp.float32)
-
-        @pl.when(z < nz - 1)
-        def _():
-            along_z(z, True, piece).wait_recv()
-            last[pieces[piece]] += zbuf[0, z, pieces[piece]].astype(jnp.float32)
-
-        @pl.when(z > 0)
-        def _():
-            along_z(z, False, piece).wait_recv()
-            last[pieces[piece]] += zbuf[1, z, pieces[piece]].astype(jnp.float32)
-
-        held[z, 3, pieces[piece]] = last[pieces[piece]].astype(jnp.bfloat16)
-
     def tail(piece):
         return remote(
             held.at[z, 3, pieces[piece]],
@@ -546,6 +559,19 @@
         )
 
     for piece in (0, 1):
+        last[pieces[piece]] = held[z, 3, pieces[piece]].astype(jnp.float32)
+
+        @pl.when(z < nz - 1)
+        def _():
+            along_z(z, True, piece).wait_recv()
+            last[pieces[piece]] += zbuf[0, z, pieces[piece]].astype(jnp.float32)
+
+        @pl.when(z > 0)
+        def _():
+            along_z(z, False, piece).wait_recv()
+            last[pieces[piece]] += zbuf[1, z, pieces[piece]].astype(jnp.float32)
+
+        held[z, 3, pieces[piece]] = last[pieces[piece]].astype(jnp.bfloat16)
         tail(piece).start()
 
     def drain(zz, _):
@@ -600,24 +626,47 @@
             DMA((3,)),
         ],
         compiler_params=pltpu.CompilerParams(
-            collective_id=1, has_side_effects=True, vmem_limit_bytes=VMEM_LIMIT
+            collective_id=1, has_side_effects=True, vmem_limit_bytes=16 * 1024 * 1024
         ),
         name="scatter",
     )(dq, dkv)
 
 
+def pack_kernel(stash, own_ids, keys, values, blk, sems):
+    rows = keys.shape[2]
+    parts = []
+    for i, source in enumerate((keys, values)):
+        part = pltpu.make_async_copy(
+            source.at[0, stash[0]], blk.at[pl.ds(i * rows, rows)], sems.at[i]
+        )
+        part.start()
+        parts.append(part)
+    lane = lax.broadcasted_iota(jnp.int32, (ID_ROWS, blk.shape[1]), 1)
+    numbers = jnp.where(lane < blk.shape[1] // 2, own_ids[0], own_ids[1])
+    blk[2 * rows :, :] = numbers.astype(jnp.float32).astype(jnp.bfloat16)
+    for part in parts:
+        part.wait()
+
+
+def packed(stash, own_ids, keys, values):
+    rows, head = keys.shape[2:]
+    return pl.pallas_call(
+        pack_kernel,
+        out_shape=jax.ShapeDtypeStruct((2 * rows + ID_ROWS, head), keys.dtype),
+        in_specs=[SMEM, SMEM, IN_HBM, IN_HBM],
+        out_specs=VMEM,
+        scratch_shapes=[DMA((2,))],
+        compiler_params=pltpu.CompilerParams(vmem_limit_bytes=4 * 1024 * 1024),
+        name="pack",
+    )(stash, own_ids, keys, values)
+
+
 def per_device(sizes, queries, keys, values, out_grad, stretch_ids, stash_slot):
     ns, nz, nx = sizes
-    stash_index = stash_slot[0]
-    key_rows = lax.dynamic_index_in_dim(keys[0], stash_index, 0, keepdims=False)
-    value_rows = lax.dynamic_index_in_dim(values[0], stash_index, 0, keepdims=False)
-    head = key_rows.shape[1]
-    lane = lax.broadcasted_iota(jnp.int32, (ID_ROWS, head), 1)
-    id_rows = jnp.where(lane < head // 2, stretch_ids[0], stretch_ids[1]).astype(jnp.bfloat16)
-    blk = jnp.concatenate([key_rows, value_rows, id_rows], axis=0)
+    head = keys.shape[3]
+    blk = packed(stash_slot, stretch_ids, keys, values)
     blocks = gathered(blk, nz, nx)
-    ids = blocks[:, 2 * key_rows.shape[0], :: head // 2].astype(jnp.int32).reshape(-1)
-    dq, dkv = attended(stash_slot, ids, stretch_ids, queries, out_grad, blocks, head)
+    dq, dkv = attended(stash_slot, stretch_ids, queries, out_grad, blocks, head)
     return scattered(dq, dkv, nz, nx, ns)[None]
 
 

time: 146 us -> 133 us (0.911)
  the two profiles are of different devices: /device:TPU:58 before, /device:TPU:48 now
where the time goes in v3:
time: 133 us; the launch traced here: 132 us
  Pallas kernels  128 us (96%)
  local copies, waits for them, and re-layouts  3.24 us (2%)
    pallas_call x1, Pallas kernels, scattered(): pl.pallas_call(functools.partial(scatter_kernel, nz, nx, ns), out_shape=j...  77.1 us
    pallas_call x1, Pallas kernels, gathered(): pl.pallas_call(functools.partial(gather_kernel, nz, nx), out_shape=jax.Sh...  37 us
    pallas_call x1, Pallas kernels, attended(): pl.pallas_call(functools.partial(attend_kernel, group, head, half, 1.0 /...  13.7 us
    unnamed x13, local copies, waits for them, and re-layouts  3.24 us

profile of v3, /device:TPU:48, one launch (start us, length us, event | category | flops | bytes accessed | tf_op | source)
XLA Modules:
  0.0 132.5 jit_solution(550769401943538678)
XLA Ops:
  0.0 0.0 copy-start
  0.7 0.0 copy-start.1
  0.8 0.9 copy-done.1
  1.7 0.0 copy-start.2
  1.7 0.9 copy-done.2
  2.6 0.0 copy-start.4
  2.6 0.7 copy-done.4
  3.3 0.0 copy-start.3
  3.3 0.0 copy-start.5
  3.3 0.7 pack.1.blk
  4.0 37.0 %gather.1.blocks = bf16[64,272,128]{2,1,0:T(8,128)(2,1)S(1)} custom-call(bf16[272,128]{1,0:T(8,128)(2,1)S(1)} %pack.1.blk), custom_call_target="tpu_custom_call" | custom-call | tf_op jit(solution)/shard_map/gather/pallas_call | solution.py:212
  41.0 0.0 copy-done
  41.0 0.0 copy-done.3
  41.0 0.0 copy-done.5
  41.0 13.7 %attend.1 = (bf16[128,512]{1,0:T(8,128)(2,1)S(1)}, bf16[64,256,128]{2,1,0:T(8,128)(2,1)S(1)}) custom-call(s32[1]{0:T(128)S(6)} %copy.8.stash, s32[2]{0:T(128)S(1)} %copy-done.5, bf16[1,8,128,512]{3,2,1,0:T(8,128)(2,1)S(1)} %copy-done, bf16[1,128,512]{2,1,0:T(8,128)(2,1)S(1)} %copy-done.3, bf16[64,272,128]{2,1,0:T(8,128)(2,1)S(1)} %gather.1.blocks), custom_call_target="tpu_custom_call" | custom-call | tf_op jit(solution)/shard_map/attend/pallas_call | solution.py:389
  54.7 77.1 %scatter.1 = bf16[128,768]{1,0:T(8,128)(2,1)S(1)} custom-call(bf16[128,512]{1,0:T(8,128)(2,1)S(1)} %get-tuple-element.7.dq, bf16[64,256,128]{2,1,0:T(8,128)(2,1)S(1)} %get-tuple-element.8.dkv), custom_call_target="tpu_custom_call" | custom-call | tf_op jit(solution)/shard_map/scatter/pallas_call | solution.py:605
  131.8 0.7 copy.9
Async XLA Ops:
  0.0 41.0 %copy-start = (bf16[1,8,128,512]{3,2,1,0:T(8,128)(2,1)S(1)}, bf16[1,8,128,512]{3,2,1,0:T(8,128)(2,1)}, u32[]{:S(2)}) copy-start(bf16[1,8,128,512]{3,2,1,0:T(8,128)(2,1)} %queries.1) | copy-start | bytes 3145732
  0.7 1.0 copy-start.1
  1.7 0.9 copy-start.2
  2.6 0.7 copy-start.4
  3.3 37.7 %copy-start.3 = (bf16[1,128,512]{2,1,0:T(8,128)(2,1)S(1)}, bf16[1,128,512]{2,1,0:T(8,128)(2,1)}, u32[]{:S(2)}) copy-start(bf16[1,128,512]{2,1,0:T(8,128)(2,1)} %grads.1) | copy-start | bytes 393220
  3.3 37.7 %copy-start.5 = (s32[2]{0:T(128)S(1)}, s32[2]{0:T(128)}, u32[]{:S(2)}) copy-start(s32[2]{0:T(128)} %own_ids.3) | copy-start | bytes 28

commit v4 on v3

--- a/solution.py
+++ b/solution.py
@@ -331,7 +331,7 @@
         deltas[p] = deltas[p] * fading + jnp.sum(e * dprob, axis=0, keepdims=True)
 
     units = tiles + 1
-    together = 3 if units % 3 == 0 else 1
+    together = 11 if units % 11 == 0 else 1
 
     def forward_step(i, _):
         for k in range(together):
@@ -656,7 +656,7 @@
         in_specs=[SMEM, SMEM, IN_HBM, IN_HBM],
         out_specs=VMEM,
         scratch_shapes=[DMA((2,))],
-        compiler_params=pltpu.CompilerParams(vmem_limit_bytes=4 * 1024 * 1024),
+        compiler_params=pltpu.CompilerParams(vmem_limit_bytes=VMEM_LIMIT),
         name="pack",
     )(stash, own_ids, keys, values)
 

time: 133 us -> 130 us (0.977)
  the two profiles are of different devices: /device:TPU:48 before, /device:TPU:56 now
where the time goes in v4:
time: 130 us
  Pallas kernels  127 us (98%)
  local copies, waits for them, and re-layouts  1.57 us (1%)
    pallas_call x1, Pallas kernels, scattered(): pl.pallas_call(functools.partial(scatter_kernel, nz, nx, ns), out_shape=j...  76.8 us
    pallas_call x1, Pallas kernels, gathered(): pl.pallas_call(functools.partial(gather_kernel, nz, nx), out_shape=jax.Sh...  37.1 us
    pallas_call x1, Pallas kernels, attended(): pl.pallas_call(functools.partial(attend_kernel, group, head, half, 1.0 /...  11.4 us

profile of v4, /device:TPU:56, one launch (start us, length us, event | category | flops | bytes accessed | tf_op | source)
XLA Modules:
  0.0 129.7 jit_solution(14175056828684014124)
XLA Ops:
  0.0 0.0 copy-start
  0.7 2.1 %pack.1.blk = bf16[272,128]{1,0:T(8,128)(2,1)} custom-call(s32[1]{0:T(128)S(6)} %copy.8.stash, s32[2]{0:T(128)} %own_ids.3, bf16[1,8,128,128]{3,2,1,0:T(8,128)(2,1)} %keys.1, bf16[1,8,128,128]{3,2,1,0:T(8,128)(2,1)} %values.1), custom_call_target="tpu_custom_call" | custom-call | tf_op jit(solution)/shard_map/pack/pallas_call | solution.py:653
  2.8 0.0 copy-start.1
  2.8 0.9 copy-done.1
  3.7 0.0 copy-start.2
  3.7 0.0 copy-start.3
  3.7 37.1 %gather.1.blocks = bf16[64,272,128]{2,1,0:T(8,128)(2,1)S(1)} custom-call(bf16[272,128]{1,0:T(8,128)(2,1)S(1)} %copy-done.1), custom_call_target="tpu_custom_call" | custom-call | tf_op jit(solution)/shard_map/gather/pallas_call | solution.py:212
  40.9 0.0 copy-done
  40.9 0.0 copy-done.2
  40.9 0.0 copy-done.3
  40.9 11.4 %attend.1 = (bf16[128,512]{1,0:T(8,128)(2,1)S(1)}, bf16[64,256,128]{2,1,0:T(8,128)(2,1)S(1)}) custom-call(s32[1]{0:T(128)S(6)} %copy.8.stash, s32[2]{0:T(128)S(1)} %copy-done.3, bf16[1,8,128,512]{3,2,1,0:T(8,128)(2,1)S(1)} %copy-done, bf16[1,128,512]{2,1,0:T(8,128)(2,1)S(1)} %copy-done.2, bf16[64,272,128]{2,1,0:T(8,128)(2,1)S(1)} %gather.1.blocks), custom_call_target="tpu_custom_call" | custom-call | tf_op jit(solution)/shard_map/attend/pallas_call | solution.py:389
  52.3 76.8 %scatter.1 = bf16[128,768]{1,0:T(8,128)(2,1)S(1)} custom-call(bf16[128,512]{1,0:T(8,128)(2,1)S(1)} %get-tuple-element.7.dq, bf16[64,256,128]{2,1,0:T(8,128)(2,1)S(1)} %get-tuple-element.8.dkv), custom_call_target="tpu_custom_call" | custom-call | tf_op jit(solution)/shard_map/scatter/pallas_call | solution.py:605
  129.0 0.7 copy.9
Async XLA Ops:
  0.0 40.9 %copy-start = (bf16[1,8,128,512]{3,2,1,0:T(8,128)(2,1)S(1)}, bf16[1,8,128,512]{3,2,1,0:T(8,128)(2,1)}, u32[]{:S(2)}) copy-start(bf16[1,8,128,512]{3,2,1,0:T(8,128)(2,1)} %queries.1) | copy-start | bytes 3145732
  2.8 0.9 copy-start.1
  3.7 37.2 %copy-start.2 = (bf16[1,128,512]{2,1,0:T(8,128)(2,1)S(1)}, bf16[1,128,512]{2,1,0:T(8,128)(2,1)}, u32[]{:S(2)}) copy-start(bf16[1,128,512]{2,1,0:T(8,128)(2,1)} %grads.1) | copy-start | bytes 393220
  3.7 37.2 %copy-start.3 = (s32[2]{0:T(128)S(1)}, s32[2]{0:T(128)}, u32[]{:S(2)}) copy-start(s32[2]{0:T(128)} %own_ids.3) | copy-start | bytes 28

commit v5 on v4

--- a/solution.py
+++ b/solution.py
@@ -21,6 +21,7 @@
 
 ID_ROWS = 16
 PIECES = 2
+SUM_PIECES = 4
 masked_score = -1e30
 
 
@@ -247,6 +248,8 @@
     q_full,
     qs,
     gs,
+    qt,
+    gt,
     tops,
     totals,
     deltas,
@@ -280,6 +283,9 @@
             cols = slice(h * head, (h + 1) * head)
             qs[p, h * half : (h + 1) * half, :] = q_full[pl.ds(base, half), cols]
             gs[p, h * half : (h + 1) * half, :] = grads[0, pl.ds(base, half), cols]
+    for p in (0, 1):
+        qt[p] = qs[p].T
+        gt[p] = gs[p].T
     tops[...] = jnp.full_like(tops, masked_score)
     totals[...] = jnp.zeros_like(totals)
     deltas[...] = jnp.zeros_like(deltas)
@@ -317,9 +323,9 @@
     def forward(u):
         p, tile = unit(u)
         mine = jnp.where(p == 0, high, low)
-        t = cross(tile_of(tile, 0), qs[p], ((1,), (1,))) * exp_scale
+        t = cross(tile_of(tile, 0), qt[p], ((1,), (0,))) * exp_scale
         t = jnp.where(gap <= mine * half - tile * 256, t, masked_score)
-        dprob = cross(tile_of(tile, 2 * half), gs[p], ((1,), (1,)))
+        dprob = cross(tile_of(tile, 2 * half), gt[p], ((1,), (0,)))
         scores[u] = t
         dprobs[u] = dprob
         old = tops[p]
@@ -398,6 +404,8 @@
             pltpu.VMEM((tokens, width), jnp.bfloat16),
             pltpu.VMEM((2, rows, head), jnp.bfloat16),
             pltpu.VMEM((2, rows, head), jnp.bfloat16),
+            pltpu.VMEM((2, head, rows), jnp.bfloat16),
+            pltpu.VMEM((2, head, rows), jnp.bfloat16),
             pltpu.VMEM((2, 1, rows), jnp.float32),
             pltpu.VMEM((2, 1, rows), jnp.float32),
             pltpu.VMEM((2, 1, rows), jnp.float32),
@@ -486,13 +494,15 @@
         held[zz, 3] = done.astype(jnp.bfloat16)
 
     pieces = (pl.ds(0, tokens), pl.ds(tokens, tokens))
+    size = 2 * tokens // SUM_PIECES
+    bits = [pl.ds(i * size, size) for i in range(SUM_PIECES)]
 
     def along_z(zz, down, piece):
         to = z - 1 if down else z + 1
         way = 0 if down else 1
         return remote(
-            held.at[zz, 3, pieces[piece]],
-            zbuf.at[way, zz, pieces[piece]],
+            held.at[zz, 3, bits[piece]],
+            zbuf.at[way, zz, bits[piece]],
             zs.at[way, zz, piece],
             zr.at[way, zz, piece],
             {Z: to},
@@ -500,15 +510,15 @@
 
     def chain(zz, down, source):
         way = 0 if down else 1
-        for piece in (0, 1):
+        for piece in range(SUM_PIECES):
 
             @pl.when(source)
             def _():
                 along_z(zz, down, piece).wait_recv()
-                joined = held[zz, 3, pieces[piece]].astype(jnp.float32) + zbuf[
-                    way, zz, pieces[piece]
+                joined = held[zz, 3, bits[piece]].astype(jnp.float32) + zbuf[
+                    way, zz, bits[piece]
                 ].astype(jnp.float32)
-                held[zz, 3, pieces[piece]] = joined.astype(jnp.bfloat16)
+                held[zz, 3, bits[piece]] = joined.astype(jnp.bfloat16)
 
             along_z(zz, down, piece).start()
 
@@ -558,17 +568,20 @@
             {SECTION: ahead},
         )
 
+    share = SUM_PIECES // 2
     for piece in (0, 1):
         last[pieces[piece]] = held[z, 3, pieces[piece]].astype(jnp.float32)
 
         @pl.when(z < nz - 1)
         def _():
-            along_z(z, True, piece).wait_recv()
+            for i in range(share * piece, share * piece + share):
+                along_z(z, True, i).wait_recv()
             last[pieces[piece]] += zbuf[0, z, pieces[piece]].astype(jnp.float32)
 
         @pl.when(z > 0)
         def _():
-            along_z(z, False, piece).wait_recv()
+            for i in range(share * piece, share * piece + share):
+                along_z(z, False, i).wait_recv()
             last[pieces[piece]] += zbuf[1, z, pieces[piece]].astype(jnp.float32)
 
         held[z, 3, pieces[piece]] = last[pieces[piece]].astype(jnp.bfloat16)
@@ -580,7 +593,7 @@
         for way in (0, 1):
             half_on(zz, way).wait_send()
             along_x(zz, way).wait_send()
-        for piece in (0, 1):
+        for piece in range(SUM_PIECES):
 
             @pl.when(zz < z)
             def _():
@@ -620,8 +633,8 @@
             DMA((2, nz)),
             DMA((2, nz)),
             DMA((2, nz)),
-            DMA((2, nz, 2)),
-            DMA((2, nz, 2)),
+            DMA((2, nz, SUM_PIECES)),
+            DMA((2, nz, SUM_PIECES)),
             DMA((3,)),
             DMA((3,)),
         ],

time: 130 us -> 130 us (level)
  no operation moved by 1% of the time
where the time goes in v5:
time: 130 us
  Pallas kernels  128 us (98%)
  local copies, waits for them, and re-layouts  1.57 us (1%)
    pallas_call x1, Pallas kernels, scattered(): pl.pallas_call(functools.partial(scatter_kernel, nz, nx, ns), out_shape=j...  77.2 us
    pallas_call x1, Pallas kernels, gathered(): pl.pallas_call(functools.partial(gather_kernel, nz, nx), out_shape=jax.Sh...  37.1 us
    pallas_call x1, Pallas kernels, attended(): pl.pallas_call(functools.partial(attend_kernel, group, head, half, 1.0 /...  11.2 us

profile of v5, /device:TPU:56, one launch (start us, length us, event | category | flops | bytes accessed | tf_op | source)
XLA Modules:
  0.0 130.0 jit_solution(9487534795772815221)
XLA Ops:
  0.0 0.0 copy-start
  0.7 2.1 %pack.1.blk = bf16[272,128]{1,0:T(8,128)(2,1)} custom-call(s32[1]{0:T(128)S(6)} %copy.8.stash, s32[2]{0:T(128)} %own_ids.3, bf16[1,8,128,128]{3,2,1,0:T(8,128)(2,1)} %keys.1, bf16[1,8,128,128]{3,2,1,0:T(8,128)(2,1)} %values.1), custom_call_target="tpu_custom_call" | custom-call | tf_op jit(solution)/shard_map/pack/pallas_call | solution.py:666
  2.8 0.0 copy-start.1
  2.8 0.9 copy-done.1
  3.7 0.0 copy-start.2
  3.7 0.0 copy-start.3
  3.7 37.1 %gather.1.blocks = bf16[64,272,128]{2,1,0:T(8,128)(2,1)S(1)} custom-call(bf16[272,128]{1,0:T(8,128)(2,1)S(1)} %copy-done.1), custom_call_target="tpu_custom_call" | custom-call | tf_op jit(solution)/shard_map/gather/pallas_call | solution.py:213
  40.9 0.0 copy-done
  40.9 0.0 copy-done.2
  40.9 0.0 copy-done.3
  40.9 11.2 %attend.1 = (bf16[128,512]{1,0:T(8,128)(2,1)S(1)}, bf16[64,256,128]{2,1,0:T(8,128)(2,1)S(1)}) custom-call(s32[1]{0:T(128)S(6)} %copy.8.stash, s32[2]{0:T(128)S(1)} %copy-done.3, bf16[1,8,128,512]{3,2,1,0:T(8,128)(2,1)S(1)} %copy-done, bf16[1,128,512]{2,1,0:T(8,128)(2,1)S(1)} %copy-done.2, bf16[64,272,128]{2,1,0:T(8,128)(2,1)S(1)} %gather.1.blocks), custom_call_target="tpu_custom_call" | custom-call | tf_op jit(solution)/shard_map/attend/pallas_call | solution.py:395
  52.1 77.2 %scatter.1 = bf16[128,768]{1,0:T(8,128)(2,1)S(1)} custom-call(bf16[128,512]{1,0:T(8,128)(2,1)S(1)} %get-tuple-element.7.dq, bf16[64,256,128]{2,1,0:T(8,128)(2,1)S(1)} %get-tuple-element.8.dkv), custom_call_target="tpu_custom_call" | custom-call | tf_op jit(solution)/shard_map/scatter/pallas_call | solution.py:618
  129.4 0.7 copy.9
Async XLA Ops:
  0.0 40.9 %copy-start = (bf16[1,8,128,512]{3,2,1,0:T(8,128)(2,1)S(1)}, bf16[1,8,128,512]{3,2,1,0:T(8,128)(2,1)}, u32[]{:S(2)}) copy-start(bf16[1,8,128,512]{3,2,1,0:T(8,128)(2,1)} %queries.1) | copy-start | bytes 3145732
  2.8 0.9 copy-start.1
  3.7 37.2 %copy-start.2 = (bf16[1,128,512]{2,1,0:T(8,128)(2,1)S(1)}, bf16[1,128,512]{2,1,0:T(8,128)(2,1)}, u32[]{:S(2)}) copy-start(bf16[1,128,512]{2,1,0:T(8,128)(2,1)} %grads.1) | copy-start | bytes 393220
  3.7 37.2 %copy-start.3 = (s32[2]{0:T(128)S(1)}, s32[2]{0:T(128)}, u32[]{:S(2)}) copy-start(s32[2]{0:T(128)} %own_ids.3) | copy-start | bytes 28
